TPU v7x, 32 devices: a whole 2x2x4 slice. The times are simulated.
32 devices in a mesh: row: 8 (over z, x), col: 4 (over y, core).
Axes of the slice: x: 2, y: 2, z: 4, core: 2. Of those that a mesh axis runs over, the one named last changes fastest.
Arguments:
- tokens: bfloat16 [64, 12288], P('row', 'col'), may hold values from -6 to 6
- past_tokens: bfloat16 [64, 12288], P('row', 'col'), may hold values from -6 to 6
- out_grad: bfloat16 [64, 12288], P('row', 'col'), may hold values from -3 to 3
- w_in: bfloat16 [12288, 24576], P('col', 'row'), may hold values from -0.0546875 to 0.0546875
- w_out: bfloat16 [24576, 12288], P('row', 'col'), may hold values from -0.0390625 to 0.0390625
Outputs:
- layer_out: bfloat16 [64, 12288], P('row', 'col')
- input_grad: bfloat16 [64, 12288], P('row', 'col')
- grad_w_in: bfloat16 [12288, 24576], P('col', 'row')
- grad_w_out: bfloat16 [24576, 12288], P('row', 'col')
All inputs are finite; a program needn't handle non-finite values.
Results may differ from a plain program's by a relative error of at most 0.005.
Values may be sent and summed in bfloat16 or wider, within the bound.
A program may use at most 128 MiB of HBM per device.

v0:
```python
import jax
import jax.numpy as jnp
from jax import lax
from jax.sharding import PartitionSpec as P


def gelu_parts(pre):
    cdf = 0.5 * (1.0 + jax.scipy.special.erf(pre * 0.7071067811865476))
    slope = cdf + pre * jnp.exp(-0.5 * pre * pre) * 0.3989422804014327
    return (pre * cdf, slope)


def local(tokens, past_tokens, out_grad, w_in, w_out):
    pre_part = jnp.dot(
        lax.all_gather(tokens, "row", axis=0, tiled=True), w_in, preferred_element_type=jnp.float32
    )
    pre_share = lax.psum_scatter(pre_part, "col", scatter_dimension=0, tiled=True)
    hidden_share = gelu_parts(pre_share)[0].astype(jnp.bfloat16)
    hidden_all = lax.all_gather(hidden_share, "col", axis=0, tiled=True)
    block = hidden_all
    layer_out = lax.psum_scatter(
        jnp.dot(block, w_out, preferred_element_type=jnp.float32),
        "row",
        scatter_dimension=0,
        tiled=True,
    ).astype(jnp.bfloat16)
    past_all, grad_all = (
        lax.all_gather(past_tokens, "row", axis=0, tiled=True),
        lax.all_gather(out_grad, "row", axis=0, tiled=True),
    )
    past_part = jnp.dot(past_all, w_in, preferred_element_type=jnp.float32)
    back_part = lax.dot_general(
        grad_all, w_out, (((1,), (1,)), ((), ())), preferred_element_type=jnp.float32
    )
    past_share, back_share = (
        lax.psum_scatter(past_part, "col", scatter_dimension=0, tiled=True),
        lax.psum_scatter(back_part, "col", scatter_dimension=0, tiled=True),
    )
    act_share, slope = gelu_parts(past_share)
    act_local = act_share.astype(jnp.bfloat16)
    grad_local = (back_share * slope).astype(jnp.bfloat16)
    act_all, hidden_grad = (
        lax.all_gather(act_local, "col", axis=0, tiled=True),
        lax.all_gather(grad_local, "col", axis=0, tiled=True),
    )
    grad_w_out = lax.dot_general(
        act_all, grad_all, (((0,), (0,)), ((), ())), preferred_element_type=jnp.float32
    ).astype(jnp.bfloat16)
    grad_w_in = lax.dot_general(
        past_all, hidden_grad, (((0,), (0,)), ((), ())), preferred_element_type=jnp.float32
    ).astype(jnp.bfloat16)
    block = hidden_grad
    input_grad = lax.psum_scatter(
        lax.dot_general(block, w_in, (((1,), (1,)), ((), ())), preferred_element_type=jnp.float32),
        "row",
        scatter_dimension=0,
        tiled=True,
    ).astype(jnp.bfloat16)
    return (layer_out, input_grad, grad_w_in, grad_w_out)


def solution(mesh):
    in_specs = (P("row", "col"), P("row", "col"), P("row", "col"), P("col", "row"), P("row", "col"))
    out_specs = (P("row", "col"), P("row", "col"), P("col", "row"), P("row", "col"))
    return jax.shard_map(local, mesh=mesh, in_specs=in_specs, out_specs=out_specs, check_vma=False)
```

profile of v0, /device:TPU:0, one launch (start us, length us, event | category | flops | bytes accessed | tf_op | source)
XLA Modules:
  0.0 301.0 jit_solution(17160969050519650466)
XLA Ops:
  7.2 0.0 copy-start
  7.2 0.0 reduce-scatter.6.cloned.1.call-start
  7.2 33.0 %all_gather.18 = bf16[64,3072]{1,0:T(8,128)(2,1)S(1)} all-gather(bf16[8,3072]{1,0:T(8,128)(2,1)} %param.5), channel_id=1, replica_groups=mesh['row'=8,'col'=4] {'row'}, dimensions={0}, use_global_device_ids=true | all-gather | bytes 442368 | tf_op jit(solution)/shard_map/all_gather | solution.py:15
  40.2 0.0 copy-start.1
  40.2 10.6 %fusion.6 = f32[64,3072]{1,0:T(8,128)} fusion(bf16[64,3072]{1,0:T(8,128)(2,1)S(1)} %all_gather.18, bf16[3072,3072]{1,0:T(8,128)(2,1)} %param.8), kind=kOutput, calls=%fused_computation.12 | convolution fusion | flops 1207959552 | bytes 20054016 | tf_op jit(solution)/shard_map/dot_general | solution.py:14
  50.8 0.0 reduce-scatter.6.cloned.1.call-update
  50.9 0.0 reduce-scatter.10.cloned.1.call-start
  50.9 0.0 copy-done
  50.9 31.0 %all_gather.20 = bf16[64,3072]{1,0:T(8,128)(2,1)S(1)} all-gather(bf16[8,3072]{1,0:T(8,128)(2,1)S(1)} %copy-done), channel_id=1, replica_groups=mesh['row'=8,'col'=4] {'row'}, dimensions={0}, use_global_device_ids=true | all-gather | bytes 442368 | tf_op jit(solution)/shard_map/all_gather | solution.py:29
  81.9 13.1 %fusion.8 = f32[64,3072]{1,0:T(8,128)} fusion(bf16[64,3072]{1,0:T(8,128)(2,1)S(1)} %all_gather.20, bf16[3072,3072]{1,0:T(8,128)(2,1)} %param.9), kind=kOutput, calls=%fused_computation.14 | convolution fusion | flops 1207959552 | bytes 20054016 | tf_op jit(solution)/shard_map/dot_general | solution.py:32
  95.0 0.0 reduce-scatter.10.cloned.1.call-update
  95.0 0.0 reduce-scatter.12.cloned.1.call-start
  95.0 0.0 copy-done.1
  95.0 31.0 %all_gather.21 = bf16[64,3072]{1,0:T(8,128)(2,1)S(1)} all-gather(bf16[8,3072]{1,0:T(8,128)(2,1)S(1)} %copy-done.1), channel_id=1, replica_groups=mesh['row'=8,'col'=4] {'row'}, dimensions={0}, use_global_device_ids=true | all-gather | bytes 442368 | tf_op jit(solution)/shard_map/all_gather | solution.py:28
  126.0 10.6 %fusion.9 = f32[64,3072]{1,0:T(8,128)} fusion(bf16[64,3072]{1,0:T(8,128)(2,1)S(1)} %all_gather.21, bf16[3072,3072]{1,0:T(8,128)(2,1)} %param.8), kind=kOutput, calls=%fused_computation.15 | convolution fusion | flops 1207959552 | bytes 20054016 | tf_op jit(solution)/shard_map/dot_general | solution.py:31
  136.6 0.0 reduce-scatter.12.cloned.1.call-update
  136.7 0.0 reduce-scatter.8.cloned.1.call-start
  136.7 0.0 reduce-scatter.6.cloned.1.call-done
  136.7 1.0 multiply_convert_fusion.1
  137.7 6.7 %all_gather.19 = bf16[64,3072]{1,0:T(8,128)(2,1)S(1)} all-gather(bf16[16,3072]{1,0:T(8,128)(2,1)S(1)} %multiply_convert_fusion.1), channel_id=1, replica_groups=mesh['row'=8,'col'=4] {'col'}, dimensions={0}, use_global_device_ids=true | all-gather | bytes 491520 | tf_op jit(solution)/shard_map/all_gather | solution.py:19
  144.4 10.8 %fusion.7 = f32[64,3072]{1,0:T(8,128)} fusion(bf16[64,3072]{1,0:T(8,128)(2,1)S(1)} %all_gather.19, bf16[3072,3072]{1,0:T(8,128)(2,1)} %param.9), kind=kOutput, calls=%fused_computation.13 | convolution fusion | flops 1207959552 | bytes 20054016 | tf_op jit(solution)/shard_map/dot_general | solution.py:22
  155.2 0.0 reduce-scatter.8.cloned.1.call-update
  155.2 0.0 reduce-scatter.14.cloned.1.call-start
  155.3 0.0 reduce-scatter.10.cloned.1.call-done
  155.3 5.8 %reduce-scatter.12.cloned.1.call-done = f32[16,3072]{1,0:T(8,128)} async-done(((f32[64,3072]{1,0:T(8,128)}), f32[16,3072]{1,0:T(8,128)}) %reduce-scatter.12.cloned.1.call-update) | async-done | bytes 196624 | tf_op jit(solution)/shard_map/reduce_scatter | solution.py:36
  161.1 1.1 multiply_convert_fusion
  162.2 6.1 %all_gather.22 = bf16[64,3072]{1,0:T(8,128)(2,1)S(1)} all-gather(bf16[16,3072]{1,0:T(8,128)(2,1)S(1)} %get-tuple-element.9), channel_id=1, replica_groups=mesh['row'=8,'col'=4] {'col'}, dimensions={0}, use_global_device_ids=true | all-gather | bytes 491520 | tf_op jit(solution)/shard_map/all_gather | solution.py:44
  168.3 13.1 %fusion.10 = f32[64,3072]{1,0:T(8,128)} fusion(bf16[64,3072]{1,0:T(8,128)(2,1)S(1)} %all_gather.22, bf16[3072,3072]{1,0:T(8,128)(2,1)} %param.8), kind=kOutput, calls=%fused_computation.16 | convolution fusion | flops 1207959552 | bytes 20054016 | tf_op jit(solution)/shard_map/dot_general | solution.py:54
  181.5 0.0 reduce-scatter.14.cloned.1.call-update
  181.5 9.5 %convert_bitcast_fusion = bf16[3072,3072]{0,1:T(8,128)(2,1)} fusion(bf16[64,3072]{1,0:T(8,128)(2,1)S(1)} %all_gather.22, bf16[64,3072]{1,0:T(8,128)(2,1)S(1)} %all_gather.21), kind=kOutput, calls=%fused_computation | convolution fusion | flops 1217396736 | bytes 19660800 | tf_op jit(solution)/shard_map/dot_general | solution.py:49
  191.0 24.6 %copy.9 = bf16[3072,3072]{1,0:T(8,128)(2,1)} copy(bf16[3072,3072]{0,1:T(8,128)(2,1)} %convert_bitcast_fusion) | data formatting | bytes 37748736
  215.6 6.7 %all_gather.23 = bf16[64,3072]{1,0:T(8,128)(2,1)S(1)} all-gather(bf16[16,3072]{1,0:T(8,128)(2,1)S(1)} %get-tuple-element.8), channel_id=1, replica_groups=mesh['row'=8,'col'=4] {'col'}, dimensions={0}, use_global_device_ids=true | all-gather | bytes 491520 | tf_op jit(solution)/shard_map/all_gather | solution.py:43
  222.4 9.5 %convolution_convert_fusion = bf16[3072,3072]{1,0:T(8,128)(2,1)} fusion(bf16[64,3072]{1,0:T(8,128)(2,1)S(1)} %all_gather.23, bf16[64,3072]{1,0:T(8,128)(2,1)S(1)} %all_gather.20), kind=kOutput, calls=%fused_computation.1 | convolution fusion | flops 1217396736 | bytes 19660800 | tf_op jit(solution)/shard_map/dot_general | solution.py:46
  231.9 0.0 reduce-scatter.8.cloned.1.call-done
  231.9 1.5 convert_element_type.25
  233.4 59.5 %reduce-scatter.14.cloned.1.call-done = f32[8,3072]{1,0:T(8,128)} async-done(((f32[64,3072]{1,0:T(8,128)}), f32[8,3072]{1,0:T(8,128)}) %reduce-scatter.14.cloned.1.call-update) | async-done | bytes 98320 | tf_op jit(solution)/shard_map/reduce_scatter | solution.py:53
  292.9 1.5 convert_element_type.27
Async XLA Ops:
  7.2 43.8 %copy-start = (bf16[8,3072]{1,0:T(8,128)(2,1)S(1)}, bf16[8,3072]{1,0:T(8,128)(2,1)}, u32[]{:S(2)}) copy-start(bf16[8,3072]{1,0:T(8,128)(2,1)} %param.7) | copy-start | bytes 147460
  7.2 129.6 %reduce-scatter.6.cloned.1.call-start = ((), (), s32[]{:S(2)}) async-start(), calls=%async_computation.5 | async-start | bytes 983040 | tf_op jit(solution)/shard_map/reduce_scatter | solution.py:17
  40.2 54.8 %copy-start.1 = (bf16[8,3072]{1,0:T(8,128)(2,1)S(1)}, bf16[8,3072]{1,0:T(8,128)(2,1)}, u32[]{:S(2)}) copy-start(bf16[8,3072]{1,0:T(8,128)(2,1)} %param.6) | copy-start | bytes 147460
  50.9 104.4 %reduce-scatter.10.cloned.1.call-start = ((), (), s32[]{:S(2)}) async-start(), calls=%async_computation.7 | async-start | bytes 983040 | tf_op jit(solution)/shard_map/reduce_scatter | solution.py:37
  95.0 66.1 %reduce-scatter.12.cloned.1.call-start = ((), (), s32[]{:S(2)}) async-start(), calls=%async_computation.8 | async-start | bytes 983040 | tf_op jit(solution)/shard_map/reduce_scatter | solution.py:36
  136.7 95.2 %reduce-scatter.8.cloned.1.call-start = ((), (), s32[]{:S(2)}) async-start(), calls=%async_computation.6 | async-start | bytes 884736 | tf_op jit(solution)/shard_map/reduce_scatter | solution.py:21
  155.2 137.7 %reduce-scatter.14.cloned.1.call-start = ((), (), s32[]{:S(2)}) async-start(), calls=%async_computation.9 | async-start | bytes 884736 | tf_op jit(solution)/shard_map/reduce_scatter | solution.py:53
Sparse Core Ops, SparseCore 0:
  51.0 24.2 reduce-scatter.5
  95.1 24.2 reduce-scatter.9
  136.8 24.2 reduce-scatter.11
  164.2 63.2 reduce-scatter.7
  230.6 62.2 reduce-scatter.13
where the time goes:
time: 302 us; the launch traced here: 301 us
  blocking collectives  114 us (38%)
  matrix products  77.3 us (26%)
  waiting for transfers between devices  65.4 us (22%)
  local copies, waits for them, and re-layouts  24.6 us (8%)
  between operations  13.8 us (5%)
  other arithmetic  5.13 us (2%)
    reduce_scatter x1, waiting for transfers between devices, local(): lax.psum_scatter(lax.dot_general(block, w_in, (((1,), (1,)), ((), ())), p...  59.5 us
    all_gather x1, blocking collectives, local(): lax.all_gather(tokens, 'row', axis=0, tiled=True)  33 us
    all_gather x1, blocking collectives, local(): lax.all_gather(out_grad, 'row', axis=0, tiled=True)  31 us
    all_gather x1, blocking collectives, local(): lax.all_gather(past_tokens, 'row', axis=0, tiled=True)  31 us
    unnamed x5, local copies, waits for them, and re-layouts  24.6 us
    dot_general x1, matrix products, local(): lax.dot_general(block, w_in, (((1,), (1,)), ((), ())), preferred_element_...  13.1 us
    dot_general x1, matrix products, local(): lax.dot_general(grad_all, w_out, (((1,), (1,)), ((), ())), preferred_elem...  13.1 us
    dot_general x1, matrix products, local(): jnp.dot(block, w_out, preferred_element_type=jnp.float32)  10.8 us
  transfers between devices with their start and end apart: 5, of which 2 were waited for; matrix products, arithmetic and copies ran while one was open for 32% of the time, Pallas kernels for 0%

commit v1 on v0

v1 whole, which is shorter than its diff:
```python
import functools

import jax
import jax.numpy as jnp
from jax import lax
from jax.experimental import pallas as pl
from jax.experimental.pallas import tpu as pltpu
from jax.sharding import PartitionSpec as P

MESH = pl.DeviceIdType.MESH
F32, BF16 = jnp.float32, jnp.bfloat16
NN = (((1,), (0,)), ((), ()))
NT = (((1,), (1,)), ((), ()))
TN = (((0,), (0,)), ((), ()))


def cdf_of(v):
    return 0.5 * (1.0 + lax.erf(v * 0.7071067811865476))


def slope_of(v, cdf):
    return cdf + v * jnp.exp(-0.5 * v * v) * 0.3989422804014327


def cols(i, width):
    return pl.ds(pl.multiple_of(i * width, width), width)


def exchange_kernel(
    nr, nc, nck,
    past_ref, grad_ref, tok_ref, win_hbm, wout_hbm,
    xpast, xgrad, act_out, hg_out, out_lo, out_ig,
    win, wout, g_past, g_grad, g_tok, xtok, hid,
    part, pair_in, y_out, y_in, halves,
    rs_all, rs_xs, rs_xr, rs_zs, rs_zr,
    win_sem, wout_sem, up_s, up_r, dn_s, dn_r, gx_s, gx_r,
    pr_s, pr_r, y_s, y_r, hv_s, hv_r, rx_s, rx_r, rz_s, rz_r,
):
    me, col = lax.axis_index("row"), lax.axis_index("col")
    nh, ny = nr // 2, nc // 2
    h, lo = me // 2, me % 2
    g, core = col // 2, col % 2
    d, ff = win.shape
    tr = past_ref.shape[0]
    t = nr * tr
    cw, dw = ff // nck, d // nck
    partner = (h * 2 + 1 - lo, col)
    mate = (me, g * 2 + 1 - core)

    def zdev(k):
        return (k * 2 + lo, col)

    def ydev(k):
        return (me, k * 2 + core)

    def rcopy(src, dst, ss, rs, dev):
        return pltpu.make_async_remote_copy(
            src_ref=src, dst_ref=dst, send_sem=ss, recv_sem=rs, device_id=dev, device_id_type=MESH
        )

    def wout_copy(i):
        s = cols(i, cw)
        return pltpu.make_async_copy(wout_hbm.at[s, :], wout.at[s, :], wout_sem.at[i])

    def win_copy(i):
        s = cols(i, cw)
        return pltpu.make_async_copy(win_hbm.at[:, s], win.at[:, s], win_sem.at[i])

    for i in range(nck):
        wout_copy(i).start()
        win_copy(i).start()

    barrier = pltpu.get_barrier_semaphore()
    for q in range(1, nh):
        pl.semaphore_signal(barrier, inc=1, device_id=zdev((h + q) % nh), device_id_type=MESH)
    for q in range(1, ny):
        pl.semaphore_signal(barrier, inc=1, device_id=ydev((g + q) % ny), device_id_type=MESH)
    pl.semaphore_signal(barrier, inc=1, device_id=partner, device_id_type=MESH)
    pl.semaphore_signal(barrier, inc=1, device_id=mate, device_id_type=MESH)
    pl.semaphore_wait(barrier, nh + ny)

    owns = (past_ref, grad_ref, tok_ref)
    gath = (g_past, g_grad, g_tok)

    def up(a, s, src, blk):
        return rcopy(src, gath[a].at[blk], up_s.at[a, s], up_r.at[a, s], zdev(jnp.minimum(h + 1, nh - 1)))

    def down(a, s, src, blk):
        return rcopy(src, gath[a].at[blk], dn_s.at[a, s], dn_r.at[a, s], zdev(jnp.maximum(h - 1, 0)))

    def across(a, k, src, blk):
        return rcopy(src, gath[a].at[blk], gx_s.at[a, k], gx_r.at[a, k], partner)

    def start_own(a):
        across(a, h, owns[a], me).start()

        @pl.when(h < nh - 1)
        def _():
            up(a, 0, owns[a], me).start()

        @pl.when(h > 0)
        def _():
            down(a, 0, owns[a], me).start()

        gath[a][me] = owns[a][...]

    def relay(a, s):
        kb = h - 1 - s

        @pl.when(kb >= 0)
        def _():
            blk = kb * 2 + lo
            src = gath[a].at[blk]
            up(a, s, src, blk).wait_recv()

            @pl.when((h < nh - 1) & (s < nh - 2))
            def _():
                up(a, jnp.minimum(s + 1, nh - 2), src, blk).start()

            across(a, kb, src, blk).start()

        ka = h + 1 + s

        @pl.when(ka <= nh - 1)
        def _():
            blk = ka * 2 + lo
            src = gath[a].at[blk]
            down(a, s, src, blk).wait_recv()

            @pl.when((h > 0) & (s < nh - 2))
            def _():
                down(a, jnp.minimum(s + 1, nh - 2), src, blk).start()

            across(a, ka, src, blk).start()

    def collect(a, x):
        def wait_one(k, _):
            blk = k * 2 + 1 - lo
            across(a, k, gath[a].at[blk], blk).wait_recv()
            return 0

        lax.fori_loop(0, nh, wait_one, 0)

        def put(i, _):
            s = cols(i, dw)
            x[:, s] = gath[a][:, :, s].astype(F32).reshape(t, dw).astype(BF16)
            return 0

        lax.fori_loop(0, nck, put, 0)

    start_own(0)
    start_own(1)
    for s in range(nh - 1):
        relay(0, s)
        relay(1, s)
    start_own(2)
    collect(0, xpast)
    collect(1, xgrad)

    def pair_copy(a, i, half):
        return rcopy(part.at[a, i, half], pair_in.at[a, i], pr_s.at[a, i], pr_r.at[a, i], mate)

    def y_copy(a, i, q):
        return rcopy(
            y_out.at[a, i], y_in.at[a, i, q - 1], y_s.at[a, i, q - 1], y_r.at[a, i, q - 1], ydev((g + q) % ny)
        )

    def pair_add(a, j):
        pair_copy(a, j, 1 - core).wait_recv()
        total = part[a, j, core] + pair_in[a, j]
        part[a, j, core] = total
        y_out[a, j] = total.astype(BF16)

    def y_start(a, j):
        for q in range(1, ny):
            y_copy(a, j, q).start()

    def y_total(a, j):
        total = part[a, j, core]
        for q in range(1, ny):
            y_copy(a, j, q).wait_recv()
            total = total + y_in[a, j, q - 1].astype(F32)
        return total

    per = -(-(nh - 1) // nck)

    def back_step(i, _):
        @pl.when(i < nck)
        def _():
            s = cols(i, cw)
            wout_copy(i).wait()
            back = lax.dot_general(xgrad[...], wout[s, :], NT, preferred_element_type=F32)
            part[0, i] = back.reshape(2, t // 2, cw)
            win_copy(i).wait()
            past = lax.dot_general(xpast[...], win[:, s], NN, preferred_element_type=F32)
            part[1, i] = past.reshape(2, t // 2, cw)
            pair_copy(0, i, 1 - core).start()
            pair_copy(1, i, 1 - core).start()
            for k in range(per):
                @pl.when(i * per + k < nh - 1)
                def _():
                    relay(2, i * per + k)

        @pl.when(i > 0)
        def _():
            pair_add(0, i - 1)
            pair_add(1, i - 1)
            y_start(0, i - 1)
            y_start(1, i - 1)

        return 0

    lax.fori_loop(0, nck + 1, back_step, 0)
    collect(2, xtok)

    def fwd_step(i, _):
        @pl.when(i < nck)
        def _():
            s = cols(i, cw)
            pre = lax.dot_general(xtok[...], win[:, s], NN, preferred_element_type=F32)
            part[2, i] = pre.reshape(2, t // 2, cw)
            pair_copy(2, i, 1 - core).start()

        @pl.when(i > 0)
        def _():
            pair_add(2, i - 1)
            y_start(2, i - 1)

        return 0

    lax.fori_loop(0, nck + 1, fwd_step, 0)

    def half_copy(a, i, k):
        return rcopy(halves.at[a, i, k], halves.at[a, i, k], hv_s.at[a, i], hv_r.at[a, i], mate)

    def back_final(j, _):
        back = y_total(0, j)
        v = y_total(1, j)
        cdf = cdf_of(v)
        halves[0, j, core] = (v * cdf).astype(BF16)
        halves[1, j, core] = (back * slope_of(v, cdf)).astype(BF16)
        half_copy(1, j, core).start()
        half_copy(0, j, core).start()
        return 0

    lax.fori_loop(0, nck, back_final, 0)

    def land(a, dst):
        def one(j, _):
            half_copy(a, j, 1 - core).wait_recv()
            dst[:, cols(j, cw)] = halves[a, j].reshape(t, cw)
            return 0

        lax.fori_loop(0, nck, one, 0)

    land(1, hg_out)

    def rx_copy(o, i):
        return rcopy(rs_xs.at[o, i], rs_xr.at[o, i], rx_s.at[o, i], rx_r.at[o, i], partner)

    def rz_copy(o, i, q):
        k = (h + q) % nh
        return rcopy(rs_zs.at[o, i, k], rs_zr.at[o, i, q - 1], rz_s.at[o, i, q - 1], rz_r.at[o, i, q - 1], zdev(k))

    def rs_loop(o, product):
        def step(i, _):
            @pl.when(i < nck)
            def _():
                rs_all[o, i] = product(i).reshape(nh, 2, tr, dw)
                rs_xs[o, i] = rs_all[o, i, :, 1 - lo].astype(BF16)
                rx_copy(o, i).start()

            @pl.when(i > 0)
            def _():
                j = i - 1
                rx_copy(o, j).wait_recv()
                total = rs_all[o, j, :, lo] + rs_xr[o, j].astype(F32)
                rs_all[o, j, :, lo] = total
                rs_zs[o, j] = total.astype(BF16)
                for q in range(1, nh):
                    rz_copy(o, j, q).start()

            return 0

        lax.fori_loop(0, nck + 1, step, 0)

    rs_loop(0, lambda i: lax.dot_general(hg_out[...], win[cols(i, dw), :], NT, preferred_element_type=F32))

    def fwd_final(j, _):
        v = y_total(2, j)
        halves[2, j, core] = (v * cdf_of(v)).astype(BF16)
        half_copy(2, j, core).start()
        return 0

    lax.fori_loop(0, nck, fwd_final, 0)
    land(2, hid)
    rs_loop(1, lambda i: lax.dot_general(hid[...], wout[:, cols(i, dw)], NN, preferred_element_type=F32))
    land(0, act_out)

    def rs_final(o, out):
        def one(j, _):
            total = rs_all[o, j, h, lo]
            for q in range(1, nh):
                rz_copy(o, j, q).wait_recv()
                total = total + rs_zr[o, j, q - 1].astype(F32)
            out[:, cols(j, dw)] = total.astype(BF16)
            return 0

        lax.fori_loop(0, nck, one, 0)

    rs_final(0, out_ig)
    rs_final(1, out_lo)

    def drain(i, _):
        for a in range(3):
            pair_copy(a, i, 1 - core).wait_send()
            half_copy(a, i, core).wait_send()
            for q in range(1, ny):
                y_copy(a, i, q).wait_send()
        for o in range(2):
            rx_copy(o, i).wait_send()
            for q in range(1, nh):
                rz_copy(o, i, q).wait_send()
        return 0

    lax.fori_loop(0, nck, drain, 0)
    for a in range(3):
        def drain_across(k, _):
            across(a, k, owns[a], me).wait_send()
            return 0

        lax.fori_loop(0, nh, drain_across, 0)
        for s in range(nh - 1):
            @pl.when((h < nh - 1) & (h - s >= 0))
            def _():
                up(a, s, owns[a], me).wait_send()

            @pl.when((h > 0) & (h + s <= nh - 1))
            def _():
                down(a, s, owns[a], me).wait_send()


def grads_kernel(act, grad, past, hg, gwo, gwi):
    gwo[...] = lax.dot_general(act[...], grad[...], TN, preferred_element_type=F32).astype(BF16)
    gwi[...] = lax.dot_general(past[...], hg[...], TN, preferred_element_type=F32).astype(BF16)


def local(nr, nc, tokens, past_tokens, out_grad, w_in, w_out):
    d, ff = w_in.shape
    tr = tokens.shape[0]
    t, nh, ny, nck = nr * tr, nr // 2, nc // 2, 6
    cw, dw = ff // nck, d // nck
    dma = pltpu.SemaphoreType.DMA
    vm = pl.BlockSpec(memory_space=pltpu.VMEM)
    hbm = pl.BlockSpec(memory_space=pl.ANY)
    q = max(ny - 1, 1)
    past_all, grad_all, act_all, hg_all, lo, ig = pl.pallas_call(
        functools.partial(exchange_kernel, nr, nc, nck),
        out_shape=[
            jax.ShapeDtypeStruct((t, d), BF16),
            jax.ShapeDtypeStruct((t, d), BF16),
            jax.ShapeDtypeStruct((t, ff), BF16),
            jax.ShapeDtypeStruct((t, ff), BF16),
            jax.ShapeDtypeStruct((tr, d), BF16),
            jax.ShapeDtypeStruct((tr, d), BF16),
        ],
        in_specs=[vm, vm, vm, hbm, hbm],
        out_specs=[vm] * 6,
        scratch_shapes=[
            pltpu.VMEM((d, ff), BF16),
            pltpu.VMEM((ff, d), BF16),
            pltpu.VMEM((nr, tr, d), BF16),
            pltpu.VMEM((nr, tr, d), BF16),
            pltpu.VMEM((nr, tr, d), BF16),
            pltpu.VMEM((t, d), BF16),
            pltpu.VMEM((t, ff), BF16),
            pltpu.VMEM((3, nck, 2, t // 2, cw), F32),
            pltpu.VMEM((3, nck, t // 2, cw), F32),
            pltpu.VMEM((3, nck, t // 2, cw), BF16),
            pltpu.VMEM((3, nck, q, t // 2, cw), BF16),
            pltpu.VMEM((3, nck, 2, t // 2, cw), BF16),
            pltpu.VMEM((2, nck, nh, 2, tr, dw), F32),
            pltpu.VMEM((2, nck, nh, tr, dw), BF16),
            pltpu.VMEM((2, nck, nh, tr, dw), BF16),
            pltpu.VMEM((2, nck, nh, tr, dw), BF16),
            pltpu.VMEM((2, nck, nh - 1, tr, dw), BF16),
            dma((nck,)), dma((nck,)),
            dma((3, nh - 1)), dma((3, nh - 1)), dma((3, nh - 1)), dma((3, nh - 1)),
            dma((3, nh)), dma((3, nh)),
            dma((3, nck)), dma((3, nck)),
            dma((3, nck, q)), dma((3, nck, q)),
            dma((3, nck)), dma((3, nck)),
            dma((2, nck)), dma((2, nck)),
            dma((2, nck, nh - 1)), dma((2, nck, nh - 1)),
        ],
        compiler_params=pltpu.CompilerParams(
            collective_id=0, has_side_effects=True, vmem_limit_bytes=66 * 1000 * 1000
        ),
    )(past_tokens, out_grad, tokens, w_in, w_out)

    tile = 128
    gwo, gwi = pl.pallas_call(
        grads_kernel,
        grid=(ff // tile,),
        out_shape=[jax.ShapeDtypeStruct((ff, d), BF16), jax.ShapeDtypeStruct((d, ff), BF16)],
        in_specs=[
            pl.BlockSpec((t, tile), lambda i: (0, i)),
            pl.BlockSpec((t, d), lambda i: (0, 0)),
            pl.BlockSpec((t, d * tile // ff), lambda i: (0, i)),
            pl.BlockSpec((t, ff), lambda i: (0, 0)),
        ],
        out_specs=[
            pl.BlockSpec((tile, d), lambda i: (i, 0)),
            pl.BlockSpec((d * tile // ff, ff), lambda i: (i, 0)),
        ],
        cost_estimate=pl.CostEstimate(flops=4 * t * d * ff, bytes_accessed=4 * d * ff, transcendentals=0),
    )(act_all, grad_all, past_all, hg_all)
    return lo, ig, gwi, gwo


def solution(mesh):
    nr, nc = mesh.shape["row"], mesh.shape["col"]
    in_specs = (P("row", "col"), P("row", "col"), P("row", "col"), P("col", "row"), P("row", "col"))
    out_specs = (P("row", "col"), P("row", "col"), P("col", "row"), P("row", "col"))
    return jax.shard_map(
        functools.partial(local, nr, nc), mesh=mesh, in_specs=in_specs, out_specs=out_specs, check_vma=False
    )
```

time: 302 us -> 97.4 us (0.32)
  blocking collectives: 114 us -> 0 us
  Pallas kernels: 0 us -> 92.1 us
  matrix products: 77.3 us -> 0 us
  waiting for transfers between devices: 65.4 us -> 0 us
  local copies, waits for them, and re-layouts: 24.6 us -> 2.84 us
  between operations: 13.8 us -> 0.64 us
  other arithmetic: 5.13 us -> 0 us
    all_gather x6 -> x0, blocking collectives: 114 us -> none  [the longest x1 33 us: local(): lax.all_gather(tokens, 'row', axis=0, tiled=True)]
    pallas_call x0 -> x2, Pallas kernels: none -> 92.1 us  [the longest x1 71.7 us: local(): pl.pallas_call(functools.partial(exchange_kernel, nr, nc, nck), out_shape...]
    dot_general x7 -> x0, matrix products: 77.3 us -> none  [the longest x1 13.1 us: local(): lax.dot_general(block, w_in, (((1,), (1,)), ((), ())), preferred_element_...]
    reduce_scatter x5 -> x0, waiting for transfers between devices: 65.3 us -> none  [the longest x1 59.5 us: local(): lax.psum_scatter(lax.dot_general(block, w_in, (((1,), (1,)), ((), ())), p...]
    unnamed x5 -> x2, local copies, waits for them, and re-layouts: 24.6 us -> 2.84 us
    convert_element_type x4 -> x0, other arithmetic: 5.13 us -> none  [the longest x1 1.52 us: local(): layer_out = lax.psum_scatter(jnp.dot(block, w_out, preferred_element_type...]
  transfers between devices with their start and end apart: 5 -> 0, of which waited for: 2 -> 0; matrix products, arithmetic and copies ran while one was open for 32% -> 0% of each run, Pallas kernels for 0% -> 0%
where the time goes in v1:
time: 97.4 us; the launch traced here: 95.6 us
  Pallas kernels  92.1 us (95%)
  local copies, waits for them, and re-layouts  2.84 us (3%)
    pallas_call x1, Pallas kernels, local(): pl.pallas_call(functools.partial(exchange_kernel, nr, nc, nck), out_shape...  71.7 us
    pallas_call x1, Pallas kernels, local(): pl.pallas_call(grads_kernel, grid=(ff // tile,), out_shape=[jax.ShapeDtyp...  20.4 us
    unnamed x2, local copies, waits for them, and re-layouts  2.84 us

profile of v1, /device:TPU:0, one launch (start us, length us, event | category | flops | bytes accessed | tf_op | source)
XLA Modules:
  0.0 95.6 jit_solution(11054319814061772930)
XLA Ops:
  0.6 71.7 %shard_map.84 = (bf16[64,3072]{1,0:T(8,128)(2,1)}, bf16[64,3072]{1,0:T(8,128)(2,1)}, bf16[64,3072]{1,0:T(8,128)(2,1)}, bf16[64,3072]{1,0:T(8,128)(2,1)}, bf16[8,...) custom-call(bf16[8,3072]{1,0:T(8,128)(2,1)} %past_ref.1, bf16[8,3072]{1,0:T(8,128)(2,1)} %grad_ref.1, bf16[8,3072]{1,0:T(8,128)(2,1)} %tok_ref.1, ...), custom_call_target="tpu_custom_call" | custom-call | tf_op jit(solution)/shard_map/pallas_call | solution.py:357
  72.3 20.4 %shard_map.85 = (bf16[3072,3072]{1,0:T(8,128)(2,1)}, bf16[3072,3072]{1,0:T(8,128)(2,1)}) custom-call(bf16[64,3072]{1,0:T(8,128)(2,1)} %get-tuple-element.14.act, bf16[64,3072]{1,0:T(8,128)(2,1)} %get-tuple-element.15.grad, bf16[64,3072]{1,0:T(8,128)(2,1)} %get-tuple-element.16.past, bf16[64,3072]{1,0:T(8,128)(2,1)} %get-tuple-element.17.hg), custom_call_target="tpu_custom_call" | custom-call | flops 2415919104 | bytes 37748736 | tf_op jit(solution)/shard_map/pallas_call | solution.py:402
  92.7 1.4 %copy.11 = bf16[8,3072]{1,0:T(8,128)(2,1)} copy(bf16[8,3072]{1,0:T(8,128)(2,1)} %get-tuple-element.24) | data formatting | bytes 98304
  94.1 1.4 %copy.12 = bf16[8,3072]{1,0:T(8,128)(2,1)} copy(bf16[8,3072]{1,0:T(8,128)(2,1)} %get-tuple-element.25) | data formatting | bytes 98304

commit v2 on v1

--- a/solution.py
+++ b/solution.py
@@ -148,13 +148,11 @@
 
         lax.fori_loop(0, nck, put, 0)
 
+    start_own(1)
+    relay(1, 0)
     start_own(0)
-    start_own(1)
-    for s in range(nh - 1):
-        relay(0, s)
+    for s in range(1, nh - 1):
         relay(1, s)
-    start_own(2)
-    collect(0, xpast)
     collect(1, xgrad)
 
     def pair_copy(a, i, half):
@@ -183,52 +181,63 @@
         return total
 
     per = -(-(nh - 1) // nck)
-
-    def back_step(i, _):
-        @pl.when(i < nck)
-        def _():
-            s = cols(i, cw)
-            wout_copy(i).wait()
-            back = lax.dot_general(xgrad[...], wout[s, :], NT, preferred_element_type=F32)
-            part[0, i] = back.reshape(2, t // 2, cw)
-            win_copy(i).wait()
-            past = lax.dot_general(xpast[...], win[:, s], NN, preferred_element_type=F32)
-            part[1, i] = past.reshape(2, t // 2, cw)
-            pair_copy(0, i, 1 - core).start()
-            pair_copy(1, i, 1 - core).start()
-            for k in range(per):
-                @pl.when(i * per + k < nh - 1)
+    spread = max(1, nck // (nh - 1))
+    lag = 2
+
+    def finish_chunk(a, j):
+        pair_add(a, j)
+        y_start(a, j)
+
+    def part_loop(a, product, behind, opens):
+        def step(i, _):
+            part[a, i] = product(i).reshape(2, t // 2, cw)
+            pair_copy(a, i, 1 - core).start()
+            if behind is not None:
+                for k in range(per):
+                    s = (i // spread) * per + k
+
+                    @pl.when((i % spread == 0) & (s < nh - 1))
+                    def _():
+                        relay(behind, s)
+
+            if opens is not None:
+                @pl.when(i == nck // 2)
                 def _():
-                    relay(2, i * per + k)
-
-        @pl.when(i > 0)
-        def _():
-            pair_add(0, i - 1)
-            pair_add(1, i - 1)
-            y_start(0, i - 1)
-            y_start(1, i - 1)
-
-        return 0
-
-    lax.fori_loop(0, nck + 1, back_step, 0)
+                    start_own(opens)
+
+            @pl.when(i >= lag)
+            def _():
+                finish_chunk(a, i - lag)
+
+            return 0
+
+        lax.fori_loop(0, nck, step, 0)
+
+    def part_tail(a):
+        def step(j, _):
+            finish_chunk(a, j)
+            return 0
+
+        lax.fori_loop(nck - lag, nck, step, 0)
+
+    def back_product(i):
+        wout_copy(i).wait()
+        return lax.dot_general(xgrad[...], wout[cols(i, cw), :], NT, preferred_element_type=F32)
+
+    def past_product(i):
+        win_copy(i).wait()
+        return lax.dot_general(xpast[...], win[:, cols(i, cw)], NN, preferred_element_type=F32)
+
+    def tok_product(i):
+        return lax.dot_general(xtok[...], win[:, cols(i, cw)], NN, preferred_element_type=F32)
+
+    part_loop(0, back_product, 0, 2)
+    collect(0, xpast)
+    part_tail(0)
+    part_loop(1, past_product, 2, None)
     collect(2, xtok)
-
-    def fwd_step(i, _):
-        @pl.when(i < nck)
-        def _():
-            s = cols(i, cw)
-            pre = lax.dot_general(xtok[...], win[:, s], NN, preferred_element_type=F32)
-            part[2, i] = pre.reshape(2, t // 2, cw)
-            pair_copy(2, i, 1 - core).start()
-
-        @pl.when(i > 0)
-        def _():
-            pair_add(2, i - 1)
-            y_start(2, i - 1)
-
-        return 0
-
-    lax.fori_loop(0, nck + 1, fwd_step, 0)
+    part_tail(1)
+    part_loop(2, tok_product, None, None)
 
     def half_copy(a, i, k):
         return rcopy(halves.at[a, i, k], halves.at[a, i, k], hv_s.at[a, i], hv_r.at[a, i], mate)
@@ -243,6 +252,7 @@
         half_copy(0, j, core).start()
         return 0
 
+    part_tail(2)
     lax.fori_loop(0, nck, back_final, 0)
 
     def land(a, dst):
@@ -262,27 +272,36 @@
         k = (h + q) % nh
         return rcopy(rs_zs.at[o, i, k], rs_zr.at[o, i, q - 1], rz_s.at[o, i, q - 1], rz_r.at[o, i, q - 1], zdev(k))
 
+    rs_lag = min(4, nck - 1)
+
+    def rs_chunk(o, j):
+        rx_copy(o, j).wait_recv()
+        total = rs_all[o, j, :, lo] + rs_xr[o, j].astype(F32)
+        rs_all[o, j, :, lo] = total
+        rs_zs[o, j] = total.astype(BF16)
+        for q in range(1, nh):
+            rz_copy(o, j, q).start()
+
     def rs_loop(o, product):
         def step(i, _):
-            @pl.when(i < nck)
-            def _():
-                rs_all[o, i] = product(i).reshape(nh, 2, tr, dw)
-                rs_xs[o, i] = rs_all[o, i, :, 1 - lo].astype(BF16)
-                rx_copy(o, i).start()
-
-            @pl.when(i > 0)
-            def _():
-                j = i - 1
-                rx_copy(o, j).wait_recv()
-                total = rs_all[o, j, :, lo] + rs_xr[o, j].astype(F32)
-                rs_all[o, j, :, lo] = total
-                rs_zs[o, j] = total.astype(BF16)
-                for q in range(1, nh):
-                    rz_copy(o, j, q).start()
-
-            return 0
-
-        lax.fori_loop(0, nck + 1, step, 0)
+            rs_all[o, i] = product(i).reshape(nh, 2, tr, dw)
+            rs_xs[o, i] = rs_all[o, i, :, 1 - lo].astype(BF16)
+            rx_copy(o, i).start()
+
+            @pl.when(i >= rs_lag)
+            def _():
+                rs_chunk(o, i - rs_lag)
+
+            return 0
+
+        lax.fori_loop(0, nck, step, 0)
+
+    def rs_tail(o):
+        def step(j, _):
+            rs_chunk(o, j)
+            return 0
+
+        lax.fori_loop(nck - rs_lag, nck, step, 0)
 
     rs_loop(0, lambda i: lax.dot_general(hg_out[...], win[cols(i, dw), :], NT, preferred_element_type=F32))
 
@@ -293,9 +312,11 @@
         return 0
 
     lax.fori_loop(0, nck, fwd_final, 0)
+    rs_tail(0)
     land(2, hid)
     rs_loop(1, lambda i: lax.dot_general(hid[...], wout[:, cols(i, dw)], NN, preferred_element_type=F32))
     land(0, act_out)
+    rs_tail(1)
 
     def rs_final(o, out):
         def one(j, _):
@@ -340,9 +361,33 @@
                 down(a, s, owns[a], me).wait_send()
 
 
-def grads_kernel(act, grad, past, hg, gwo, gwi):
-    gwo[...] = lax.dot_general(act[...], grad[...], TN, preferred_element_type=F32).astype(BF16)
-    gwi[...] = lax.dot_general(past[...], hg[...], TN, preferred_element_type=F32).astype(BF16)
+def grads_kernel(steps, act, grad, past, hg, lo_in, ig_in, gwo, gwi, lo_out, ig_out, so, si, sem_o, sem_i):
+    lo_out[...] = lo_in[...]
+    ig_out[...] = ig_in[...]
+    to, ti = so.shape[0] // steps, si.shape[0] // steps
+
+    def copy_o(i):
+        return pltpu.make_async_copy(so.at[cols(i, to), :], gwo.at[cols(i, to), :], sem_o.at[i])
+
+    def copy_i(i):
+        return pltpu.make_async_copy(si.at[cols(i, ti), :], gwi.at[cols(i, ti), :], sem_i.at[i])
+
+    def step(i, _):
+        o, k = cols(i, to), cols(i, ti)
+        so[o, :] = lax.dot_general(act[:, o], grad[...], TN, preferred_element_type=F32).astype(BF16)
+        copy_o(i).start()
+        si[k, :] = lax.dot_general(past[:, k], hg[...], TN, preferred_element_type=F32).astype(BF16)
+        copy_i(i).start()
+        return 0
+
+    lax.fori_loop(0, steps, step, 0)
+
+    def drain(i, _):
+        copy_o(i).wait()
+        copy_i(i).wait()
+        return 0
+
+    lax.fori_loop(0, steps, drain, 0)
 
 
 def local(nr, nc, tokens, past_tokens, out_grad, w_in, w_out):
@@ -398,23 +443,20 @@
         ),
     )(past_tokens, out_grad, tokens, w_in, w_out)
 
-    tile = 128
-    gwo, gwi = pl.pallas_call(
-        grads_kernel,
-        grid=(ff // tile,),
-        out_shape=[jax.ShapeDtypeStruct((ff, d), BF16), jax.ShapeDtypeStruct((d, ff), BF16)],
-        in_specs=[
-            pl.BlockSpec((t, tile), lambda i: (0, i)),
-            pl.BlockSpec((t, d), lambda i: (0, 0)),
-            pl.BlockSpec((t, d * tile // ff), lambda i: (0, i)),
-            pl.BlockSpec((t, ff), lambda i: (0, 0)),
+    gwo, gwi, lo, ig = pl.pallas_call(
+        functools.partial(grads_kernel, nck),
+        out_shape=[
+            jax.ShapeDtypeStruct((ff, d), BF16),
+            jax.ShapeDtypeStruct((d, ff), BF16),
+            jax.ShapeDtypeStruct((tr, d), BF16),
+            jax.ShapeDtypeStruct((tr, d), BF16),
         ],
-        out_specs=[
-            pl.BlockSpec((tile, d), lambda i: (i, 0)),
-            pl.BlockSpec((d * tile // ff, ff), lambda i: (i, 0)),
-        ],
+        in_specs=[vm] * 6,
+        out_specs=[hbm, hbm, vm, vm],
+        scratch_shapes=[pltpu.VMEM((ff, d), BF16), pltpu.VMEM((d, ff), BF16), dma((nck,)), dma((nck,))],
         cost_estimate=pl.CostEstimate(flops=4 * t * d * ff, bytes_accessed=4 * d * ff, transcendentals=0),
-    )(act_all, grad_all, past_all, hg_all)
+        compiler_params=pltpu.CompilerParams(vmem_limit_bytes=60 * 1000 * 1000),
+    )(act_all, grad_all, past_all, hg_all, lo, ig)
     return lo, ig, gwi, gwo
 
 

time: 97.4 us -> 82.9 us (0.85); the launches traced: 95.6 us -> 82.7 us
  Pallas kernels: 92.1 us -> 82.1 us
  local copies, waits for them, and re-layouts: 2.84 us -> 0 us
    pallas_call x1, Pallas kernels: 20.4 us -> 15.4 us  [local(): pl.pallas_call(functools.partial(grads_kernel, nck), out_shape=[jax.Shape...]
    pallas_call x1, Pallas kernels: 71.7 us -> 66.7 us  [local(): pl.pallas_call(functools.partial(exchange_kernel, nr, nc, nck), out_shape...]
    unnamed x2 -> x0, local copies, waits for them, and re-layouts: 2.84 us -> none
where the time goes in v2:
time: 82.9 us; the launch traced here: 82.7 us
  Pallas kernels  82.1 us (99%)
    pallas_call x1, Pallas kernels, local(): pl.pallas_call(functools.partial(exchange_kernel, nr, nc, nck), out_shape...  66.7 us
    pallas_call x1, Pallas kernels, local(): pl.pallas_call(functools.partial(grads_kernel, nck), out_shape=[jax.Shape...  15.4 us

profile of v2, /device:TPU:0, one launch (start us, length us, event | category | flops | bytes accessed | tf_op | source)
XLA Modules:
  0.0 82.7 jit_solution(7089157709055104675)
XLA Ops:
  0.6 66.7 %shard_map.84 = (bf16[64,3072]{1,0:T(8,128)(2,1)}, bf16[64,3072]{1,0:T(8,128)(2,1)}, bf16[64,3072]{1,0:T(8,128)(2,1)}, bf16[64,3072]{1,0:T(8,128)(2,1)}, bf16[8,...) custom-call(bf16[8,3072]{1,0:T(8,128)(2,1)} %past_ref.1, bf16[8,3072]{1,0:T(8,128)(2,1)} %grad_ref.1, bf16[8,3072]{1,0:T(8,128)(2,1)} %tok_ref.1, ...), custom_call_target="tpu_custom_call" | custom-call | tf_op jit(solution)/shard_map/pallas_call | solution.py:402
  67.3 15.4 %shard_map.85 = (bf16[3072,3072]{1,0:T(8,128)(2,1)}, bf16[3072,3072]{1,0:T(8,128)(2,1)}, bf16[8,3072]{1,0:T(8,128)(2,1)}, bf16[8,3072]{1,0:T(8,128)(2,1)}) custom-call(bf16[64,3072]{1,0:T(8,128)(2,1)} %get-tuple-element.14.act, bf16[64,3072]{1,0:T(8,128)(2,1)} %get-tuple-element.15.grad, bf16[64,3072]{1,0:T(8,128)(2,1)} %get-tuple-element.16.past, ...), custom_call_target="tpu_custom_call" | custom-call | flops 2415919104 | bytes 37748736 | tf_op jit(solution)/shard_map/pallas_call | solution.py:446
